TPU v7x, 32 devices: a whole 2x2x4 slice. The times are simulated.
32 devices in a mesh: py: 4 (over z), px: 4 (over y, x), shift: 2 (over core).
Axes of the slice: x: 2, y: 2, z: 4, core: 2. Of those that a mesh axis runs over, the one named last changes fastest.
Arguments:
- right_side: float32 [512, 256, 256], P(('shift', 'py'), 'px'), parts along dimension 0, may hold values from -6 to 6
- first_guess: float32 [512, 256, 256], P(('shift', 'py'), 'px'), parts along dimension 0, may hold values from -6 to 6
- mass_term: float32 [512, 256, 256], P(('shift', 'py'), 'px'), parts along dimension 0, may hold values from 0.1 to 0.9
Outputs:
- corrected: float32 [512, 256, 256], P(('shift', 'py'), 'px'), parts along dimension 0
- remaining: float32 [512, 256, 256], P(('shift', 'py'), 'px'), parts along dimension 0
There are 2 independent parts, one for each index of `shift`. A program takes and returns all parts, laid end to end along the dimension named above; each array names one. Nothing has to cross between parts.
All inputs are finite; a program needn't handle non-finite values.
Results may differ from a plain program's by a relative error of at most 0.000031.
Values sent between devices are 32-bit elements.
A program may use at most 128 MiB of HBM per device.

v0:
```python
import functools

import jax
import jax.numpy as jnp
from jax import lax
from jax.experimental import pallas as pl
from jax.experimental.pallas import tpu as pltpu
from jax.sharding import PartitionSpec as P

RATIO = 4
BEFORE = 2
AFTER = 3
INNER = 9
DAMP = 0.8
LANES = 128
PAD = 8


def kernel(
    sizes, counts, rhs_hbm, guess_hbm, mass_hbm, out_hbm, rem_hbm,
    u3, rhs3, d3, w2, rem3, tmp, cu2, cr2, cw2, hb,
    recv, send, crecv, csend, in_sem, out_sem, send_sem, recv_sem, csend_sem, crecv_sem,
):
    ny, nx, halves = sizes
    cy, cx = ny // RATIO, nx // RATIO
    pitch, cpitch = nx + 2 * PAD, cx + 2 * PAD
    n_py, n_px = counts
    py, px = lax.axis_index("py"), lax.axis_index("px")
    targets = (
        {"py": lax.rem(py + 1, n_py)},
        {"py": lax.rem(py + n_py - 1, n_py)},
        {"px": lax.rem(px + 1, n_px)},
        {"px": lax.rem(px + n_px - 1, n_px)},
    )
    u = u3.reshape(halves * 2 * (ny + 2) * pitch, LANES)
    rhs = rhs3.reshape(halves * ny * nx, LANES)
    d = d3.reshape(halves * ny * nx, LANES)
    rem = rem3.reshape(halves * ny * nx, LANES)

    loads = []
    for h in range(halves):
        lanes = pl.ds(h * LANES, LANES)
        loads.append((
            pltpu.make_async_copy(
                guess_hbm.at[:, :, lanes],
                u3.at[h, 0, pl.ds(1, ny), pl.ds(PAD, nx), :], in_sem.at[h, 0]),
            pltpu.make_async_copy(mass_hbm.at[:, :, lanes], d3.at[h], in_sem.at[h, 1]),
            pltpu.make_async_copy(rhs_hbm.at[:, :, lanes], rhs3.at[h], in_sem.at[h, 2]),
        ))
    for k in range(3):
        for h in range(halves):
            loads[h][k].start()

    barrier = pltpu.get_barrier_semaphore()
    for target in targets:
        pl.semaphore_signal(barrier, inc=1, device_id=target, device_id_type=pl.DeviceIdType.MESH)

    def ub(h, pp, y):
        return pl.multiple_of(((h * 2 + pp) * (ny + 2) + y + 1) * pitch + PAD, 8)

    def fb(h, y):
        return pl.multiple_of((h * ny + y) * nx, 8)

    def cub(h, pp, y):
        return pl.multiple_of(((h * 2 + pp) * (cy + 2) + y + 1) * cpitch + PAD, 8)

    def cfb(h, y):
        return pl.multiple_of((h * cy + y) * cx, 8)

    side = jnp.zeros((PAD, LANES), jnp.float32)
    for h in range(halves):
        for pp in range(2):
            for y in (-1, ny):
                u[pl.ds(ub(h, pp, y), nx), :] = jnp.zeros((nx, LANES), jnp.float32)
            for y in (-1, cy):
                cu2[pl.ds(cub(h, pp, y), cx), :] = jnp.zeros((cx, LANES), jnp.float32)

            def clear(y, _, h=h, pp=pp):
                u[pl.ds(ub(h, pp, y) - PAD, PAD), :] = side
                u[pl.ds(ub(h, pp, y) + nx, PAD), :] = side
                return 0

            lax.fori_loop(0, ny, clear, 0, unroll=4)

            def cclear(y, _, h=h, pp=pp):
                cu2[pl.ds(cub(h, pp, y) - PAD, PAD), :] = side
                cu2[pl.ds(cub(h, pp, y) + cx, PAD), :] = side
                return 0

            lax.fori_loop(0, cy, cclear, 0, unroll=4)

    pl.semaphore_wait(barrier, 4)

    def edges(array, base, step, h, pp, rows, columns):
        first = base(h, pp, 0)
        return (
            array[pl.ds(base(h, pp, rows - 1), columns), :],
            array[pl.ds(first, columns), :],
            array[pl.ds(first + columns - 1, rows, stride=step), :],
            array[pl.ds(first, rows, stride=step), :],
        )

    def copies(e, h, coarse):
        s, r, ss, rs = (csend, crecv, csend_sem, crecv_sem) if coarse else (send, recv, send_sem, recv_sem)
        return [
            pltpu.make_async_remote_copy(
                src_ref=s.at[e, h, k], dst_ref=r.at[e, h, k],
                send_sem=ss.at[e, h, k], recv_sem=rs.at[e, h, k],
                device_id=targets[k], device_id_type=pl.DeviceIdType.MESH)
            for k in range(4)
        ]

    started = []

    def exchange(e, h, pp, coarse=False):
        if coarse:
            cells = edges(cu2, cub, cpitch, h, pp, cy, cx)
        else:
            cells = edges(u, ub, pitch, h, pp, ny, nx)
        buffer = csend if coarse else send
        for k in range(4):
            buffer[e, h, k] = cells[k]
        out = copies(e, h, coarse)
        for k in (2, 3, 0, 1):
            out[k].start()
        started.append(out)

    def arrived(e, h, coarse=False):
        for copy in copies(e, h, coarse):
            copy.wait_recv()

    def around(b):
        return (u[pl.ds(b - pitch, nx), :] + u[pl.ds(b + pitch, nx), :]) + (
            u[pl.ds(b - 1, nx), :] + u[pl.ds(b + 1, nx), :])

    def sweep(h, pp):
        def body(y, _):
            b = ub(h, pp, y)
            f = pl.ds(fb(h, y), nx)
            u[pl.ds(ub(h, 1 - pp, y), nx), :] = (1.0 - DAMP) * u[pl.ds(b, nx), :] + w2[f, :] * (
                rhs[f, :] + around(b))
            return 0

        lax.fori_loop(0, ny, body, 0, unroll=2)

    def add_edges(array, base, step, weights, wbase, h, pp, rows, columns, values):
        first, wfirst = base(h, pp, 0), wbase(h, 0)
        places = (
            (pl.ds(first, columns), pl.ds(wfirst, columns)),
            (pl.ds(base(h, pp, rows - 1), columns), pl.ds(wbase(h, rows - 1), columns)),
            (pl.ds(first, rows, stride=step), pl.ds(wfirst, rows, stride=columns)),
            (pl.ds(first + columns - 1, rows, stride=step),
             pl.ds(wfirst + columns - 1, rows, stride=columns)),
        )
        for (place, wplace), value in zip(places, values):
            if weights is not None:
                value = weights[wplace, :] * value
            array[place, :] = array[place, :] + value

    def fold(array, start, size):
        total = array[pl.ds(start, size, stride=RATIO), :]
        for j in range(1, RATIO):
            total = total + array[pl.ds(start + j, size, stride=RATIO), :]
        return total * (1.0 / RATIO)

    def masses(h):
        def body(row, _):
            total = jnp.zeros((nx, LANES), jnp.float32)
            for j in range(RATIO):
                f = pl.ds(fb(h, row * RATIO + j), nx)
                m = d[f, :]
                total = total + m
                m = 4.0 + m
                d[f, :] = m
                w2[f, :] = DAMP / m
            t = pl.multiple_of(row * nx, 8)
            tmp[pl.ds(t, nx), :] = total
            cw2[pl.ds(cfb(h, row), cx), :] = DAMP / (4.0 + fold(tmp, t, cx))
            return 0

        lax.fori_loop(0, cy, body, 0)

    for h in range(halves):
        loads[h][0].wait()
        exchange(0, h, 0)
    for h in range(halves):
        loads[h][1].wait()
        masses(h)
        loads[h][2].wait()
        sweep(h, 0)
    pp = 0
    for e in range(BEFORE):
        pp = 1 - pp
        for h in range(halves):
            arrived(e, h)
            add_edges(u, ub, pitch, w2, fb, h, pp, ny, nx, [recv[e, h, k] for k in range(4)])
            exchange(e + 1, h, pp)
            if e + 1 < BEFORE:
                sweep(h, pp)

    def defect(h):
        def body(row, _):
            total = jnp.zeros((nx, LANES), jnp.float32)
            for j in range(RATIO):
                y = row * RATIO + j
                b = ub(h, pp, y)
                f = pl.ds(fb(h, y), nx)
                total = total + (rhs[f, :] + around(b) - d[f, :] * u[pl.ds(b, nx), :])
            t = pl.multiple_of(row * nx, 8)
            tmp[pl.ds(t, nx), :] = total
            cr2[pl.ds(cfb(h, row), cx), :] = fold(tmp, t, cx)
            return 0

        lax.fori_loop(0, cy, body, 0)

    for h in range(halves):
        defect(h)
    cpp = 0
    flat = recv.reshape((BEFORE + AFTER + 1) * halves * 4 * nx, LANES)
    for h in range(halves):
        arrived(BEFORE, h)
        values = [fold(flat, ((BEFORE * halves + h) * 4 + k) * nx, cx) for k in range(4)]
        add_edges(cr2, lambda h, pp, y: cfb(h, y), cx, None, cfb, h, 0, cy, cx, values)

        def start(row, _, h=h):
            f = pl.ds(cfb(h, row), cx)
            cu2[pl.ds(cub(h, 0, row), cx), :] = cw2[f, :] * cr2[f, :]
            return 0

        lax.fori_loop(0, cy, start, 0, unroll=4)
        exchange(0, h, 0, True)

    def csweep(h, pp):
        def body(y, _):
            b = cub(h, pp, y)
            f = pl.ds(cfb(h, y), cx)
            total = (cu2[pl.ds(b - cpitch, cx), :] + cu2[pl.ds(b + cpitch, cx), :]) + (
                cu2[pl.ds(b - 1, cx), :] + cu2[pl.ds(b + 1, cx), :])
            cu2[pl.ds(cub(h, 1 - pp, y), cx), :] = (1.0 - DAMP) * cu2[pl.ds(b, cx), :] + cw2[f, :] * (
                cr2[f, :] + total)
            return 0

        lax.fori_loop(0, cy, body, 0, unroll=4)

    for e in range(INNER - 1):
        for h in range(halves):
            csweep(h, cpp)
        cpp = 1 - cpp
        for h in range(halves):
            arrived(e, h, True)
            add_edges(cu2, cub, cpitch, cw2, cfb, h, cpp, cy, cx, [crecv[e, h, k] for k in range(4)])
            exchange(e + 1, h, cpp, True)

    for h in range(halves):
        def correct(row, _, h=h):
            t = pl.multiple_of(row * nx, 8)
            c = cu2[pl.ds(cub(h, cpp, row), cx), :]
            for j in range(RATIO):
                tmp[pl.ds(t + j, cx, stride=RATIO), :] = c
            c = tmp[pl.ds(t, nx), :]
            for j in range(RATIO):
                place = pl.ds(ub(h, pp, row * RATIO + j), nx)
                u[place, :] = u[place, :] + c
            return 0

        lax.fori_loop(0, cy, correct, 0)
        sweep(h, pp)
    pp = 1 - pp
    for h in range(halves):
        arrived(INNER - 1, h, True)
        values = []
        for k in range(4):
            c = crecv[INNER - 1, h, k]
            at = (h * 4 + k) * nx
            for j in range(RATIO):
                hb[pl.ds(at + j, cx, stride=RATIO), :] = c
            values.append(recv[BEFORE, h, k] + hb[pl.ds(at, nx), :])
        add_edges(u, ub, pitch, w2, fb, h, pp, ny, nx, values)
        exchange(BEFORE + 1, h, pp)
        sweep(h, pp)
    outs = []
    for e in range(BEFORE + 1, BEFORE + AFTER):
        pp = 1 - pp
        for h in range(halves):
            arrived(e, h)
            add_edges(u, ub, pitch, w2, fb, h, pp, ny, nx, [recv[e, h, k] for k in range(4)])
            exchange(e + 1, h, pp)
            if e + 1 < BEFORE + AFTER:
                sweep(h, pp)
            else:
                outs.append(pltpu.make_async_copy(
                    u3.at[h, pp, pl.ds(1, ny), pl.ds(PAD, nx), :],
                    out_hbm.at[:, :, pl.ds(h * LANES, LANES)], out_sem.at[h, 0]))
                outs[-1].start()

    for h in range(halves):
        def left(y, _, h=h):
            b = ub(h, pp, y)
            f = pl.ds(fb(h, y), nx)
            rem[f, :] = rhs[f, :] + around(b) - d[f, :] * u[pl.ds(b, nx), :]
            return 0

        lax.fori_loop(0, ny, left, 0, unroll=2)
    e = BEFORE + AFTER
    for h in range(halves):
        arrived(e, h)
        add_edges(rem, lambda h, pp, y: fb(h, y), nx, None, fb, h, 0, ny, nx,
                  [recv[e, h, k] for k in range(4)])
        outs.append(pltpu.make_async_copy(
            rem3.at[h], rem_hbm.at[:, :, pl.ds(h * LANES, LANES)], out_sem.at[h, 1]))
        outs[-1].start()
    for group in started:
        for copy in group:
            copy.wait_send()
    for copy in outs:
        copy.wait()


def shards(right_side, first_guess, mass_term):
    ny, nx, members = right_side.shape
    halves = members // LANES
    cy, cx = ny // RATIO, nx // RATIO
    fine, coarse = BEFORE + AFTER + 1, INNER
    vmem = lambda *shape: pltpu.VMEM(shape, jnp.float32)
    dma = lambda *shape: pltpu.SemaphoreType.DMA(shape)
    counts = (lax.axis_size("py"), lax.axis_size("px"))
    return pl.pallas_call(
        functools.partial(kernel, (ny, nx, halves), counts),
        out_shape=[jax.ShapeDtypeStruct(right_side.shape, jnp.float32)] * 2,
        in_specs=[pl.BlockSpec(memory_space=pl.ANY)] * 3,
        out_specs=[pl.BlockSpec(memory_space=pl.ANY)] * 2,
        scratch_shapes=[
            vmem(halves, 2, ny + 2, nx + 2 * PAD, LANES),
            vmem(halves, ny, nx, LANES),
            vmem(halves, ny, nx, LANES),
            vmem(halves * ny * nx, LANES),
            vmem(halves, ny, nx, LANES),
            vmem(cy * nx, LANES),
            vmem(halves * 2 * (cy + 2) * (cx + 2 * PAD), LANES),
            vmem(halves * cy * cx, LANES),
            vmem(halves * cy * cx, LANES),
            vmem(halves * 4 * nx, LANES),
            vmem(fine, halves, 4, nx, LANES),
            vmem(fine, halves, 4, nx, LANES),
            vmem(coarse, halves, 4, cx, LANES),
            vmem(coarse, halves, 4, cx, LANES),
            dma(halves, 3),
            dma(halves, 2),
            dma(fine, halves, 4),
            dma(fine, halves, 4),
            dma(coarse, halves, 4),
            dma(coarse, halves, 4),
        ],
        compiler_params=pltpu.CompilerParams(
            collective_id=0, has_side_effects=True, vmem_limit_bytes=50 * 1024 * 1024),
        name="two_grid",
    )(right_side, first_guess, mass_term)


def solution(mesh):
    spec = P(("shift", "py"), "px", None)
    return jax.shard_map(
        shards, mesh=mesh, in_specs=(spec,) * 3, out_specs=(spec,) * 2, check_vma=False)
```

profile of v0, /device:TPU:0, one launch (start us, length us, event | category | flops | bytes accessed | tf_op | source)
XLA Modules:
  0.0 76.7 jit_solution(2032077028746334331)
XLA Ops:
  0.6 69.1 %two_grid.1 = (f32[64,64,256]{2,1,0:T(8,128)}, f32[64,64,256]{2,1,0:T(8,128)}) custom-call(f32[64,64,256]{2,1,0:T(8,128)} %rhs_hbm.1, f32[64,64,256]{2,1,0:T(8,128)} %guess_hbm.1, f32[64,64,256]{2,1,0:T(8,128)} %mass_hbm.1), custom_call_target="tpu_custom_call" | custom-call | tf_op jit(solution)/shard_map/two_grid/pallas_call | solution.py:327
  69.8 0.0 copy-start
  69.8 4.8 %copy.7 = f32[64,64,256]{2,1,0:T(8,128)} copy(f32[64,64,256]{2,1,0:T(8,128)} %get-tuple-element.4) | data formatting | bytes 8388608
  74.6 0.0 copy-done
  74.6 2.0 %copy.8 = f32[64,64,256]{2,1,0:T(8,128)} copy(f32[64,64,256]{2,1,0:T(8,128)S(1)} %copy-done) | data formatting | bytes 8388608
Async XLA Ops:
  69.8 4.9 %copy-start = (f32[64,64,256]{2,1,0:T(8,128)S(1)}, f32[64,64,256]{2,1,0:T(8,128)}, u32[]{:S(2)}) copy-start(f32[64,64,256]{2,1,0:T(8,128)} %get-tuple-element.5) | copy-start | bytes 12582916
where the time goes:
time: 76.8 us; the launch traced here: 76.7 us
  Pallas kernels  69.1 us (90%)
  local copies, waits for them, and re-layouts  6.87 us (9%)
    pallas_call x1, Pallas kernels, shards(): pl.pallas_call(functools.partial(kernel, (ny, nx, halves), counts), out_s...  69.1 us
    unnamed x4, local copies, waits for them, and re-layouts  6.87 us

commit v1 on v0

--- a/solution.py
+++ b/solution.py
@@ -326,9 +326,9 @@
     counts = (lax.axis_size("py"), lax.axis_size("px"))
     return pl.pallas_call(
         functools.partial(kernel, (ny, nx, halves), counts),
-        out_shape=[jax.ShapeDtypeStruct(right_side.shape, jnp.float32)] * 2,
+        out_shape=[vmem(*right_side.shape)] * 2,
         in_specs=[pl.BlockSpec(memory_space=pl.ANY)] * 3,
-        out_specs=[pl.BlockSpec(memory_space=pl.ANY)] * 2,
+        out_specs=[pl.BlockSpec(memory_space=pltpu.VMEM)] * 2,
         scratch_shapes=[
             vmem(halves, 2, ny + 2, nx + 2 * PAD, LANES),
             vmem(halves, ny, nx, LANES),
@@ -352,7 +352,7 @@
             dma(coarse, halves, 4),
         ],
         compiler_params=pltpu.CompilerParams(
-            collective_id=0, has_side_effects=True, vmem_limit_bytes=50 * 1024 * 1024),
+            collective_id=0, has_side_effects=True, vmem_limit_bytes=44 * 1024 * 1024),
         name="two_grid",
     )(right_side, first_guess, mass_term)
 

time: 76.8 us -> 72.9 us (0.949)
  local copies, waits for them, and re-layouts: 6.87 us -> 4.03 us
  Pallas kernels: 69.1 us -> 68.1 us
    unnamed x4 -> x2, local copies, waits for them, and re-layouts: 6.87 us -> 4.03 us
    pallas_call x1, Pallas kernels: 69.1 us -> 68.1 us  [shards(): pl.pallas_call(functools.partial(kernel, (ny, nx, halves), counts), out_s...]
where the time goes in v1:
time: 72.9 us; the launch traced here: 72.8 us
  Pallas kernels  68.1 us (93%)
  local copies, waits for them, and re-layouts  4.03 us (6%)
    pallas_call x1, Pallas kernels, shards(): pl.pallas_call(functools.partial(kernel, (ny, nx, halves), counts), out_s...  68.1 us
    unnamed x2, local copies, waits for them, and re-layouts  4.03 us

profile of v1, /device:TPU:0, one launch (start us, length us, event | category | flops | bytes accessed | tf_op | source)
XLA Modules:
  0.0 72.8 jit_solution(10258257788974666078)
XLA Ops:
  0.6 68.1 %two_grid.1 = (f32[64,64,256]{2,1,0:T(8,128)S(1)}, f32[64,64,256]{2,1,0:T(8,128)S(1)}) custom-call(f32[64,64,256]{2,1,0:T(8,128)} %rhs_hbm.1, f32[64,64,256]{2,1,0:T(8,128)} %guess_hbm.1, f32[64,64,256]{2,1,0:T(8,128)} %mass_hbm.1), custom_call_target="tpu_custom_call" | custom-call | tf_op jit(solution)/shard_map/two_grid/pallas_call | solution.py:327
  68.8 2.0 %copy.7 = f32[64,64,256]{2,1,0:T(8,128)} copy(f32[64,64,256]{2,1,0:T(8,128)S(1)} %get-tuple-element.2) | data formatting | bytes 8388608
  70.8 2.0 %copy.8 = f32[64,64,256]{2,1,0:T(8,128)} copy(f32[64,64,256]{2,1,0:T(8,128)S(1)} %get-tuple-element.3) | data formatting | bytes 8388608
